TPU v7x, 32 devices: a whole 2x2x4 slice. The times are simulated.
32 devices in a mesh: grp: 2 (over core), row: 4 (over z), col: 4 (over y, x).
Axes of the slice: x: 2, y: 2, z: 4, core: 2. Of those that a mesh axis runs over, the one named last changes fastest.
Arguments:
- ainv_anc: bfloat16 [6144, 6144], P(('grp', 'row'), 'col'), may hold values from -12 to 12
- l_upper: bfloat16 [6144, 1024], P(('grp', 'row'), 'col'), may hold values from -0.078125 to 0.078125
- mask_upper: int32 [4, 24], replicated, may hold values from 0 to 1, as said below
- dinv_upper: float32 [256, 1024], P(None, 'col'), may hold values from -6 to 6
- l_lower: bfloat16 [6144, 1024], P(('grp', 'row'), 'col'), may hold values from -0.078125 to 0.078125
- mask_lower: int32 [4, 24], replicated, may hold values from 0 to 1, as said below
- parent: int32 [4], replicated, may hold values from 0 to 3
- lp_lower: bfloat16 [256, 1024], P(None, 'col'), may hold values from -0.375 to 0.375
- dinv_lower: float32 [256, 1024], P(None, 'col'), may hold values from -6 to 6
Outputs:
- x_upper: bfloat16 [6144, 1024], P(('grp', 'row'), 'col')
- diag_upper: bfloat16 [256, 1024], P(None, 'col')
- y_lower: bfloat16 [6144, 1024], P(('grp', 'row'), 'col')
- y_parent: bfloat16 [256, 1024], P(None, 'col')
- diag_lower: bfloat16 [256, 1024], P(None, 'col')
Inputs may be any that keep to these rules, and one draw needn't show every extreme that they name: mask_upper[u, a] is 1 where ancestor block a lies in the structure of upper supernode u. mask_lower[l, a] is 1 where ancestor block a lies in the structure of lower supernode l. parent[l] is the upper supernode whose columns hold lower supernode l's parent block.
All inputs are finite; a program needn't handle non-finite values.
Results may differ from a plain program's by a relative error of at most 0.0095.
Values may be sent and summed in bfloat16 or wider, within the bound.
A program may use at most 128 MiB of HBM per device.

v0:
```python
import jax
import jax.numpy as jnp
from jax import lax
from jax.sharding import PartitionSpec as P

B = 256


def masked_shard(factor, pattern, block_from, node_from):
    height, breadth = factor.shape
    blocks = height // B
    supernodes = breadth // B
    picked = lax.dynamic_slice(pattern, (node_from, block_from), (supernodes, blocks))
    shaped = factor.reshape(blocks, B, supernodes, B)
    keeping = (jnp.transpose(picked) > 0)[:, None, :, None]
    return jnp.where(keeping, shaped, jnp.zeros((), factor.dtype)).reshape(height, breadth)


def column_panel(masked):
    every_row = lax.all_gather(masked, ("grp", "row"), axis=0, tiled=True)
    gathered = lax.all_to_all(every_row, "col", split_axis=0, concat_axis=1, tiled=True)
    return gathered


def summed_panel(ancestor, masked):
    gathered = column_panel(masked)
    partial_value = jnp.dot(ancestor, gathered, preferred_element_type=jnp.float32)
    return lax.psum_scatter(partial_value, "col", scatter_dimension=1, tiled=True)


def on_device(
    ainv_anc, l_upper, mask_upper, dinv_upper, l_lower, mask_lower, parent, lp_lower, dinv_lower
):
    height = ainv_anc.shape[0]
    breadth = l_upper.shape[1]
    per_device = breadth // B
    block_from = lax.axis_index(("grp", "row")) * (height // B)
    node_from = lax.axis_index("col") * per_device
    upper_masked = masked_shard(l_upper, mask_upper, block_from, node_from)
    x_upper = (-summed_panel(ainv_anc, upper_masked)).astype(jnp.bfloat16)
    upper_terms = jnp.einsum(
        "akb,akc->bkc",
        upper_masked.reshape(height, per_device, B),
        x_upper.reshape(height, per_device, B),
        preferred_element_type=jnp.float32,
    ).reshape(B, breadth)
    upper_total = lax.psum(upper_terms, ("grp", "row"))
    diag_upper = (dinv_upper - upper_total).astype(jnp.bfloat16)
    lower_masked = masked_shard(l_lower, mask_lower, block_from, node_from)
    lower_sum = summed_panel(ainv_anc, lower_masked)
    x_rows, diag_rows = (
        lax.all_gather(x_upper, "col", axis=1, tiled=True),
        lax.all_gather(diag_upper, "col", axis=1, tiled=True),
    )
    parents_here = lax.dynamic_slice_in_dim(parent, node_from, per_device)
    lower_parts, crossed_parts, own_parts = ([], [], [])
    member = 0
    chosen = lax.dynamic_slice_in_dim(x_rows, parents_here[member] * B, B, 1)
    coupling = jnp.dot(chosen, lp_lower, preferred_element_type=jnp.float32)
    y_block = (-(lower_sum + coupling)).astype(jnp.bfloat16)
    lower_parts.append(y_block)
    crossed_parts.append(
        jnp.einsum("ab,ac->bc", chosen, lower_masked, preferred_element_type=jnp.float32)
    )
    own_parts.append(
        jnp.einsum("ab,ac->bc", lower_masked, y_block, preferred_element_type=jnp.float32)
    )
    y_lower = lower_parts[0]
    crossed_sum, own_sum = lax.psum((crossed_parts[0], own_parts[0]), ("grp", "row"))
    parent_parts, diag_parts = ([], [])
    member = 0
    parent_diag = lax.dynamic_slice_in_dim(diag_rows, parents_here[member] * B, B, 1)
    parent_terms = jnp.dot(parent_diag, lp_lower, preferred_element_type=jnp.float32)
    y_block = (-(crossed_sum + parent_terms)).astype(jnp.bfloat16)
    back_terms = jnp.einsum("cb,cd->bd", lp_lower, y_block, preferred_element_type=jnp.float32)
    diag_block = dinv_lower - own_sum - back_terms
    parent_parts.append(y_block)
    diag_parts.append(diag_block.astype(jnp.bfloat16))
    y_parent = parent_parts[0]
    diag_lower = diag_parts[0]
    return (x_upper, diag_upper, y_lower, y_parent, diag_lower)


def solution(mesh):
    return jax.shard_map(
        on_device,
        mesh=mesh,
        in_specs=(
            P(("grp", "row"), "col"),
            P(("grp", "row"), "col"),
            P(),
            P(None, "col"),
            P(("grp", "row"), "col"),
            P(),
            P(),
            P(None, "col"),
            P(None, "col"),
        ),
        out_specs=(
            P(("grp", "row"), "col"),
            P(None, "col"),
            P(("grp", "row"), "col"),
            P(None, "col"),
            P(None, "col"),
        ),
        check_vma=False,
    )
```

profile of v0, /device:TPU:0, one launch (start us, length us, event | category | flops | bytes accessed | tf_op | source)
XLA Modules:
  0.0 344.0 jit_solution(8300862386639493324)
XLA Ops:
  7.2 0.0 copy-start
  7.2 0.0 all-gather.4.cloned.1.call-start
  7.2 0.9 compare_bitcast_fusion
  8.2 0.1 broadcast_in_dim.28
  8.3 1.9 broadcast_select_fusion.1
  10.2 0.0 all-gather.4.cloned.1.call-update
  10.2 0.0 all-gather.6.cloned.1.call-start
  10.2 0.1 broadcast_in_dim.32
  10.3 1.9 broadcast_select_fusion
  12.3 0.0 all-gather.6.cloned.1.call-update
  12.3 0.0 reduce-scatter.3.cloned.1.call-start
  12.3 39.0 %all-gather.4.cloned.1.call-done = bf16[6144,256]{1,0:T(8,128)(2,1)} async-done(((bf16[768,256]{1,0:T(8,128)(2,1)}), bf16[6144,256]{1,0:T(8,128)(2,1)}) %all-gather.4.cloned.1.call-update) | async-done | bytes 3145744 | tf_op jit(solution)/shard_map/all_gather | solution.py:20
  51.3 42.6 %all_to_all.38 = bf16[4,1536,256]{2,1,0:T(8,128)(2,1)} all-to-all(bf16[4,1536,256]{2,1,0:T(8,128)(2,1)} %bitcast.43), channel_id=1, replica_groups=mesh['grp'=2,'row'=4,'col'=4] {'col'}, dimensions={0} | all-to-all | bytes 6291456 | tf_op jit(solution)/shard_map/all_to_all | solution.py:21
  93.9 4.6 %copy.26 = bf16[1536,4,256]{0,2,1:T(8,128)(2,1)} copy(bf16[1536,4,256]{2,0,1:T(8,128)(2,1)} %bitcast.40) | data formatting | bytes 6291456 | tf_op jit(solution)/shard_map/all_to_all | solution.py:21
  98.5 0.0 copy-done
  98.5 6.2 %convolution_bitcast_fusion.1 = f32[768,1024]{0,1:T(8,128)} fusion(bf16[1536,1024]{0,1:T(8,128)(2,1)} %bitcast.44, bf16[768,1536]{1,0:T(8,128)(2,1)S(1)} %copy-done), kind=kOutput, calls=%fused_computation.1 | convolution fusion | flops 2415919104 | bytes 8650752 | tf_op jit(solution)/shard_map/dot_general | solution.py:27
  104.7 0.0 reduce-scatter.3.cloned.1.call-update
  104.7 0.0 reduce-scatter.5.cloned.1.call-start
  104.8 0.0 all-gather.6.cloned.1.call-done
  104.8 57.3 %all_to_all.39 = bf16[4,1536,256]{2,1,0:T(8,128)(2,1)} all-to-all(bf16[4,1536,256]{2,1,0:T(8,128)(2,1)} %bitcast.42), channel_id=1, replica_groups=mesh['grp'=2,'row'=4,'col'=4] {'col'}, dimensions={0} | all-to-all | bytes 6291456 | tf_op jit(solution)/shard_map/all_to_all | solution.py:21
  162.1 4.6 %copy.28 = bf16[1536,4,256]{0,2,1:T(8,128)(2,1)} copy(bf16[1536,4,256]{2,0,1:T(8,128)(2,1)} %bitcast.41) | data formatting | bytes 6291456 | tf_op jit(solution)/shard_map/all_to_all | solution.py:21
  166.7 6.3 %convolution_bitcast_fusion = f32[768,1024]{0,1:T(8,128)} fusion(bf16[1536,1024]{0,1:T(8,128)(2,1)} %bitcast.45, bf16[768,1536]{1,0:T(8,128)(2,1)S(1)} %copy-done), kind=kOutput, calls=%fused_computation | convolution fusion | flops 2415919104 | bytes 8650752 | tf_op jit(solution)/shard_map/dot_general | solution.py:27
  173.0 0.0 copy-start.6
  173.0 0.0 copy-start.3
  173.0 0.0 copy-start.1
  173.0 0.0 reduce-scatter.5.cloned.1.call-update
  173.0 0.0 all-gather.8.cloned.1.call-start
  173.1 5.7 %reduce-scatter.3.cloned.1.call-done = f32[768,256]{0,1:T(8,128)} async-done(((f32[768,1024]{0,1:T(8,128)}), f32[768,256]{0,1:T(8,128)}) %reduce-scatter.3.cloned.1.call-update) | async-done | bytes 786448 | tf_op jit(solution)/shard_map/reduce_scatter | solution.py:28
  178.8 1.9 negate_convert_fusion
  180.7 0.0 all-gather.8.cloned.1.call-update
  180.7 0.0 copy-start.2
  180.7 0.0 all-reduce.3.cloned.1.call-start
  180.8 0.0 copy-done.6
  180.8 0.6 dynamic_slice.17
  182.0 0.0 copy-done.3
  182.1 2.0 convolution_bitcast_fusion.2
  184.0 41.5 %reduce-scatter.5.cloned.1.call-done = f32[768,256]{0,1:T(8,128)} async-done(((f32[768,1024]{0,1:T(8,128)}), f32[768,256]{0,1:T(8,128)}) %reduce-scatter.5.cloned.1.call-update) | async-done | bytes 786448 | tf_op jit(solution)/shard_map/reduce_scatter | solution.py:28
  225.6 33.1 %all-gather.8.cloned.1.call-done = bf16[768,1024]{0,1:T(8,128)(2,1)} async-done(((bf16[768,256]{0,1:T(8,128)(2,1)}), bf16[768,1024]{0,1:T(8,128)(2,1)}) %all-gather.8.cloned.1.call-update) | async-done | bytes 1572880 | tf_op jit(solution)/shard_map/all_gather | solution.py:52
  258.7 1.6 fusion.1
  260.3 0.0 copy-done.1
  260.3 1.0 fusion.13
  261.3 2.0 fusion.6
  263.3 0.0 copy-start.4
  263.3 0.0 all-reduce.3.cloned.1.call-update
  263.4 1.8 copy.27
  265.2 0.0 copy-done.2
  265.2 0.9 copy.31
  266.1 0.9 copy.33
  267.0 54.4 %all-reduce.3.cloned.1.call-done = (f32[256,256]{0,1:T(8,128)}, f32[256,256]{1,0:T(8,128)}, f32[256,256]{1,0:T(8,128)}) async-done(((f32[256,256]{0,1:T(8,128)}, f32[256,256]{1,0:T(8,128)}, f32[256,256]{1,0:T(8,128)}), (f32[256,256]{0,1:T(8,128)}, f32[256,256]{1,0:T(8,128)}, f32[256,256]{1,0:T(8,128)})) %all-reduce.3.cloned.1.call-update) | async-done | bytes 786448 | tf_op jit(solution)/shard_map/psum | solution.py:47
  321.4 1.1 subtract_convert_fusion
  322.5 0.8 copy.32
  323.3 10.7 %all_gather.15 = bf16[256,1024]{0,1:T(8,128)(2,1)S(1)} all-gather(bf16[256,256]{0,1:T(8,128)(2,1)S(1)} %subtract_convert_fusion), channel_id=1, replica_groups=mesh['grp'=2,'row'=4,'col'=4] {'col'}, dimensions={1}, use_global_device_ids=true | all-gather | bytes 655360 | tf_op jit(solution)/shard_map/all_gather | solution.py:53
  333.9 1.2 fusion.5
  335.2 0.0 copy-start.5
  335.2 0.0 copy-done.4
  335.2 2.0 fusion.4
  337.2 0.0 copy-done.5
  (2 shorter events, 0.0 us)
Async XLA Ops:
  7.2 91.4 %copy-start = (bf16[768,1536]{1,0:T(8,128)(2,1)S(1)}, bf16[768,1536]{1,0:T(8,128)(2,1)}, u32[]{:S(2)}) copy-start(bf16[768,1536]{1,0:T(8,128)(2,1)} %param.9) | copy-start | bytes 7077892
  7.2 44.1 %all-gather.4.cloned.1.call-start = ((), (), s32[]{:S(2)}) async-start(), calls=%async_computation.4 | async-start | bytes 3538944 | tf_op jit(solution)/shard_map/all_gather | solution.py:20
  10.2 94.6 %all-gather.6.cloned.1.call-start = ((), (), s32[]{:S(2)}) async-start(), calls=%async_computation.6 | async-start | bytes 3538944 | tf_op jit(solution)/shard_map/all_gather | solution.py:20
  12.3 166.5 %reduce-scatter.3.cloned.1.call-start = ((), (), s32[]{:S(2)}) async-start(), calls=%async_computation.5 | async-start | bytes 3932160 | tf_op jit(solution)/shard_map/reduce_scatter | solution.py:28
  104.7 120.8 %reduce-scatter.5.cloned.1.call-start = ((), (), s32[]{:S(2)}) async-start(), calls=%async_computation.7 | async-start | bytes 3932160 | tf_op jit(solution)/shard_map/reduce_scatter | solution.py:28
  173.0 7.8 %copy-start.6 = (s32[4]{0:T(128)S(1)}, s32[4]{0:T(128)}, u32[]{:S(2)}) copy-start(s32[4]{0:T(128)} %param.15) | copy-start | bytes 52
  173.0 9.0 %copy-start.3 = (bf16[768,256]{1,0:T(8,128)(2,1)S(1)}, bf16[768,256]{1,0:T(8,128)(2,1)}, u32[]{:S(2)}) copy-start(bf16[768,256]{1,0:T(8,128)(2,1)} %broadcast_select_fusion.1) | copy-start | bytes 1179652
  173.0 87.3 %copy-start.1 = (bf16[768,256]{1,0:T(8,128)(2,1)S(1)}, bf16[768,256]{1,0:T(8,128)(2,1)}, u32[]{:S(2)}) copy-start(bf16[768,256]{1,0:T(8,128)(2,1)} %broadcast_select_fusion) | copy-start | bytes 1179652
  173.0 85.6 %all-gather.8.cloned.1.call-start = ((), (), s32[]{:S(2)}) async-start(), calls=%async_computation.8 | async-start | bytes 1966080 | tf_op jit(solution)/shard_map/all_gather | solution.py:52
  180.7 84.5 %copy-start.2 = (bf16[768,256]{0,1:T(8,128)(2,1)S(1)}, bf16[768,256]{0,1:T(8,128)(2,1)}, u32[]{:S(2)}) copy-start(bf16[768,256]{0,1:T(8,128)(2,1)} %negate_convert_fusion) | copy-start | bytes 1179652
  180.7 140.7 %all-reduce.3.cloned.1.call-start = ((), (), s32[]{:S(2)}) async-start(), calls=%async_computation.9 | async-start | bytes 1572864 | tf_op jit(solution)/shard_map/psum | solution.py:47
  263.3 71.9 %copy-start.4 = (bf16[256,256]{1,0:T(8,128)(2,1)S(1)}, bf16[256,256]{1,0:T(8,128)(2,1)}, u32[]{:S(2)}) copy-start(bf16[256,256]{1,0:T(8,128)(2,1)} %param.16) | copy-start | bytes 393220
  335.2 2.0 copy-start.5
Sparse Core Ops, SparseCore 0:
  10.3 40.9 all-gather.3
  52.9 37.1 all-gather.5
  104.9 73.8 reduce-scatter.2
  181.6 43.8 reduce-scatter.4
  227.8 30.8 all-gather.7
  263.5 57.9 all-reduce.2
where the time goes:
time: 345 us; the launch traced here: 344 us
  waiting for transfers between devices  174 us (50%)
  blocking collectives  111 us (32%)
  matrix products  22.3 us (6%)
  between operations  14.9 us (4%)
  local copies, waits for them, and re-layouts  14.5 us (4%)
  other arithmetic  7.74 us (2%)
    all_to_all x2, blocking collectives, column_panel(): lax.all_to_all(every_row, 'col', split_axis=0, concat_axis=1, tiled=True)  99.9 us
    psum x1, waiting for transfers between devices, on_device(): upper_total = lax.psum(upper_terms, ('grp', 'row'))  54.4 us
    reduce_scatter x2, waiting for transfers between devices, summed_panel(): lax.psum_scatter(partial_value, 'col', scatter_dimension=1, tiled=True)  47.2 us
    all_gather x2, waiting for transfers between devices, column_panel(): every_row = lax.all_gather(masked, ('grp', 'row'), axis=0, tiled=True)  39 us
    all_gather x1, waiting for transfers between devices, on_device(): lax.all_gather(x_upper, 'col', axis=1, tiled=True)  33.1 us
    dot_general x2, matrix products, summed_panel(): jnp.dot(ancestor, gathered, preferred_element_type=jnp.float32)  12.5 us
    all_gather x1, blocking collectives, on_device(): lax.all_gather(diag_upper, 'col', axis=1, tiled=True)  10.7 us
    all_to_all x2, local copies, waits for them, and re-layouts, column_panel(): lax.all_to_all(every_row, 'col', split_axis=0, concat_axis=1, tiled=True)  9.26 us
  transfers between devices with their start and end apart: 6, of which 5 were waited for; matrix products, arithmetic and copies ran while one was open for 9% of the time, Pallas kernels for 0%

commit v1 on v0

--- a/solution.py
+++ b/solution.py
@@ -44,7 +44,7 @@
         x_upper.reshape(height, per_device, B),
         preferred_element_type=jnp.float32,
     ).reshape(B, breadth)
-    upper_total = lax.psum(upper_terms, ("grp", "row"))
+    upper_total = lax.psum(lax.psum(upper_terms, "row"), "grp")
     diag_upper = (dinv_upper - upper_total).astype(jnp.bfloat16)
     lower_masked = masked_shard(l_lower, mask_lower, block_from, node_from)
     lower_sum = summed_panel(ainv_anc, lower_masked)

time: 345 us -> 388 us (1.12)
  waiting for transfers between devices: 174 us -> 218 us
    psum x1 -> x3, waiting for transfers between devices: 54.4 us -> 87.7 us  [the longest x1 45.8 us: on_device(): lax.psum((crossed_parts[0], own_parts[0]), ('grp', 'row'))]
    reduce_scatter x2, waiting for transfers between devices: 47.2 us -> 58.5 us  [summed_panel(): lax.psum_scatter(partial_value, 'col', scatter_dimension=1, tiled=True)]
  transfers between devices with their start and end apart: 6 -> 8, of which waited for: 5 -> 7; matrix products, arithmetic and copies ran while one was open for 9% -> 9% of each run, Pallas kernels for 0% -> 0%
where the time goes in v1:
time: 388 us; the launch traced here: 387 us
  waiting for transfers between devices  218 us (56%)
  blocking collectives  112 us (29%)
  matrix products  21.2 us (5%)
  between operations  14.9 us (4%)
  local copies, waits for them, and re-layouts  13.8 us (4%)
  other arithmetic  6.94 us (2%)
    all_to_all x2, blocking collectives, column_panel(): lax.all_to_all(every_row, 'col', split_axis=0, concat_axis=1, tiled=True)  99.9 us
    reduce_scatter x2, waiting for transfers between devices, summed_panel(): lax.psum_scatter(partial_value, 'col', scatter_dimension=1, tiled=True)  58.5 us
    psum x1, waiting for transfers between devices, on_device(): lax.psum((crossed_parts[0], own_parts[0]), ('grp', 'row'))  45.8 us
    psum x2, waiting for transfers between devices, on_device(): upper_total = lax.psum(lax.psum(upper_terms, 'row'), 'grp')  42 us
    all_gather x2, waiting for transfers between devices, column_panel(): every_row = lax.all_gather(masked, ('grp', 'row'), axis=0, tiled=True)  38.9 us
    all_gather x1, waiting for transfers between devices, on_device(): lax.all_gather(x_upper, 'col', axis=1, tiled=True)  32.6 us
    dot_general x2, matrix products, summed_panel(): jnp.dot(ancestor, gathered, preferred_element_type=jnp.float32)  12.4 us
    all_gather x1, blocking collectives, on_device(): lax.all_gather(diag_upper, 'col', axis=1, tiled=True)  11.7 us
  transfers between devices with their start and end apart: 8, of which 7 were waited for; matrix products, arithmetic and copies ran while one was open for 9% of the time, Pallas kernels for 0%

profile of v1, /device:TPU:0, one launch (start us, length us, event | category | flops | bytes accessed | tf_op | source)
XLA Modules:
  0.0 387.1 jit_solution(417148724091128572)
XLA Ops:
  7.2 0.0 copy-start
  7.2 0.0 all-gather.4.cloned.1.call-start
  7.2 0.9 compare_bitcast_fusion
  8.2 0.1 broadcast_in_dim.28
  8.3 1.9 broadcast_select_fusion.1
  10.2 0.0 all-gather.4.cloned.1.call-update
  10.2 0.0 all-gather.6.cloned.1.call-start
  10.2 0.1 broadcast_in_dim.32
  10.3 1.9 broadcast_select_fusion
  12.3 0.0 all-gather.6.cloned.1.call-update
  12.3 0.0 reduce-scatter.3.cloned.1.call-start
  12.4 38.9 %all-gather.4.cloned.1.call-done = bf16[6144,256]{1,0:T(8,128)(2,1)} async-done(((bf16[768,256]{1,0:T(8,128)(2,1)}), bf16[6144,256]{1,0:T(8,128)(2,1)}) %all-gather.4.cloned.1.call-update) | async-done | bytes 3145744 | tf_op jit(solution)/shard_map/all_gather | solution.py:20
  51.3 42.6 %all_to_all.38 = bf16[4,1536,256]{2,1,0:T(8,128)(2,1)} all-to-all(bf16[4,1536,256]{2,1,0:T(8,128)(2,1)} %bitcast.43), channel_id=1, replica_groups=mesh['grp'=2,'row'=4,'col'=4] {'col'}, dimensions={0} | all-to-all | bytes 6291456 | tf_op jit(solution)/shard_map/all_to_all | solution.py:21
  93.9 4.6 %copy.26 = bf16[1536,4,256]{0,2,1:T(8,128)(2,1)} copy(bf16[1536,4,256]{2,0,1:T(8,128)(2,1)} %bitcast.40) | data formatting | bytes 6291456 | tf_op jit(solution)/shard_map/all_to_all | solution.py:21
  98.5 0.0 copy-done
  98.5 6.2 %convolution_bitcast_fusion.1 = f32[768,1024]{0,1:T(8,128)} fusion(bf16[1536,1024]{0,1:T(8,128)(2,1)} %bitcast.45, bf16[768,1536]{1,0:T(8,128)(2,1)S(1)} %copy-done), kind=kOutput, calls=%fused_computation.1 | convolution fusion | flops 2415919104 | bytes 8650752 | tf_op jit(solution)/shard_map/dot_general | solution.py:27
  104.7 0.0 reduce-scatter.3.cloned.1.call-update
  104.8 0.0 all-reduce.5.cloned.1.call-start
  104.8 0.0 all-gather.6.cloned.1.call-done
  104.8 57.3 %all_to_all.39 = bf16[4,1536,256]{2,1,0:T(8,128)(2,1)} all-to-all(bf16[4,1536,256]{2,1,0:T(8,128)(2,1)} %bitcast.42), channel_id=1, replica_groups=mesh['grp'=2,'row'=4,'col'=4] {'col'}, dimensions={0} | all-to-all | bytes 6291456 | tf_op jit(solution)/shard_map/all_to_all | solution.py:21
  162.1 0.0 copy-start.4
  162.1 4.7 %copy.28 = bf16[1536,4,256]{0,2,1:T(8,128)(2,1)} copy(bf16[1536,4,256]{2,0,1:T(8,128)(2,1)} %bitcast.41) | data formatting | bytes 6291456 | tf_op jit(solution)/shard_map/all_to_all | solution.py:21
  166.8 12.0 %reduce-scatter.3.cloned.1.call-done = f32[768,256]{0,1:T(8,128)} async-done(((f32[768,1024]{0,1:T(8,128)}), f32[768,256]{0,1:T(8,128)}) %reduce-scatter.3.cloned.1.call-update) | async-done | bytes 786448 | tf_op jit(solution)/shard_map/reduce_scatter | solution.py:28
  178.8 1.2 negate_convert_fusion
  180.0 0.0 copy-start.2
  180.0 0.0 copy-done.4
  180.0 1.0 convolution_bitcast_fusion.2
  181.0 0.0 all-reduce.5.cloned.1.call-update
  181.0 0.0 reduce-scatter.5.cloned.1.call-start
  181.0 6.2 %convolution_bitcast_fusion = f32[768,1024]{0,1:T(8,128)} fusion(bf16[1536,1024]{0,1:T(8,128)(2,1)} %bitcast.44, bf16[768,1536]{1,0:T(8,128)(2,1)S(1)} %copy-done), kind=kOutput, calls=%fused_computation | convolution fusion | flops 2415919104 | bytes 8650752 | tf_op jit(solution)/shard_map/dot_general | solution.py:27
  187.3 0.0 copy-done.2
  187.3 0.0 copy-start.7
  187.3 0.0 copy-start.5
  187.3 0.0 copy-start.1
  187.3 0.0 reduce-scatter.5.cloned.1.call-update
  187.3 0.0 all-gather.8.cloned.1.call-start
  187.4 0.5 all-gather.8.cloned.1.call-update
  187.9 0.0 all-reduce.7.cloned.1.call-start
  187.9 1.1 copy.27
  189.0 0.0 copy-done.7
  189.0 0.6 dynamic_slice.17
  190.3 0.0 copy-done.3
  190.3 0.9 copy.31
  191.2 26.0 %all-reduce.5.cloned.1.call-done = f32[256,256]{0,1:T(8,128)} async-done(((f32[256,256]{0,1:T(8,128)}), f32[256,256]{0,1:T(8,128)}) %all-reduce.5.cloned.1.call-update) | async-done | bytes 262160 | tf_op jit(solution)/shard_map/psum | solution.py:47
  217.2 0.0 all-reduce.7.cloned.1.call-update
  217.2 0.0 all-reduce.9.cloned.1.call-start
  217.3 46.6 %reduce-scatter.5.cloned.1.call-done = f32[768,256]{0,1:T(8,128)} async-done(((f32[768,1024]{0,1:T(8,128)}), f32[768,256]{0,1:T(8,128)}) %reduce-scatter.5.cloned.1.call-update) | async-done | bytes 786448 | tf_op jit(solution)/shard_map/reduce_scatter | solution.py:28
  263.8 32.6 %all-gather.8.cloned.1.call-done = bf16[768,1024]{0,1:T(8,128)(2,1)} async-done(((bf16[768,256]{0,1:T(8,128)(2,1)}), bf16[768,1024]{0,1:T(8,128)(2,1)}) %all-gather.8.cloned.1.call-update) | async-done | bytes 1572880 | tf_op jit(solution)/shard_map/all_gather | solution.py:52
  296.4 0.0 copy-done.5
  296.4 1.6 fusion.1
  298.0 0.0 copy-done.1
  298.0 2.0 fusion.6
  300.0 1.0 fusion.13
  301.0 0.0 all-reduce.9.cloned.1.call-update
  301.0 16.0 %all-reduce.7.cloned.1.call-done = f32[256,256]{0,1:T(8,128)} async-done(((f32[256,256]{0,1:T(8,128)}), f32[256,256]{0,1:T(8,128)}) %all-reduce.7.cloned.1.call-update) | async-done | bytes 262160 | tf_op jit(solution)/shard_map/psum | solution.py:47
  317.0 1.0 subtract_convert_fusion
  318.0 0.8 copy.32
  318.7 11.7 %all_gather.15 = bf16[256,1024]{0,1:T(8,128)(2,1)} all-gather(bf16[256,256]{0,1:T(8,128)(2,1)S(1)} %subtract_convert_fusion), channel_id=1, replica_groups=mesh['grp'=2,'row'=4,'col'=4] {'col'}, dimensions={1}, use_global_device_ids=true | all-gather | bytes 655360 | tf_op jit(solution)/shard_map/all_gather | solution.py:53
  330.4 0.9 copy.33
  331.3 45.8 %all-reduce.9.cloned.1.call-done = (f32[256,256]{1,0:T(8,128)}, f32[256,256]{1,0:T(8,128)}) async-done(((f32[256,256]{1,0:T(8,128)}, f32[256,256]{1,0:T(8,128)}), (f32[256,256]{1,0:T(8,128)}, f32[256,256]{1,0:T(8,128)})) %all-reduce.9.cloned.1.call-update) | async-done | bytes 524304 | tf_op jit(solution)/shard_map/psum | solution.py:69
  377.0 1.2 fusion.5
  378.3 0.0 copy-start.6
  378.3 2.0 fusion.4
  380.3 0.0 copy-done.6
  (3 shorter events, 0.0 us)
Async XLA Ops:
  7.2 91.4 %copy-start = (bf16[768,1536]{1,0:T(8,128)(2,1)S(1)}, bf16[768,1536]{1,0:T(8,128)(2,1)}, u32[]{:S(2)}) copy-start(bf16[768,1536]{1,0:T(8,128)(2,1)} %param.9) | copy-start | bytes 7077892
  7.2 44.1 %all-gather.4.cloned.1.call-start = ((), (), s32[]{:S(2)}) async-start(), calls=%async_computation.4 | async-start | bytes 3538944 | tf_op jit(solution)/shard_map/all_gather | solution.py:20
  10.2 94.6 %all-gather.6.cloned.1.call-start = ((), (), s32[]{:S(2)}) async-start(), calls=%async_computation.8 | async-start | bytes 3538944 | tf_op jit(solution)/shard_map/all_gather | solution.py:20
  12.3 166.5 %reduce-scatter.3.cloned.1.call-start = ((), (), s32[]{:S(2)}) async-start(), calls=%async_computation.5 | async-start | bytes 3932160 | tf_op jit(solution)/shard_map/reduce_scatter | solution.py:28
  104.8 112.4 %all-reduce.5.cloned.1.call-start = ((), (), s32[]{:S(2)}) async-start(), calls=%async_computation.6 | async-start | bytes 524288 | tf_op jit(solution)/shard_map/psum | solution.py:47
  162.1 17.9 %copy-start.4 = (bf16[768,256]{1,0:T(8,128)(2,1)S(1)}, bf16[768,256]{1,0:T(8,128)(2,1)}, u32[]{:S(2)}) copy-start(bf16[768,256]{1,0:T(8,128)(2,1)} %broadcast_select_fusion.1) | copy-start | bytes 1179652
  180.0 7.3 %copy-start.2 = (bf16[768,256]{0,1:T(8,128)(2,1)}, bf16[768,256]{0,1:T(8,128)(2,1)S(1)}, u32[]{:S(2)}) copy-start(bf16[768,256]{0,1:T(8,128)(2,1)S(1)} %negate_convert_fusion) | copy-start | bytes 1179652
  181.0 82.8 %reduce-scatter.5.cloned.1.call-start = ((), (), s32[]{:S(2)}) async-start(), calls=%async_computation.9 | async-start | bytes 3932160 | tf_op jit(solution)/shard_map/reduce_scatter | solution.py:28
  187.3 1.8 copy-start.7
  187.3 109.1 %copy-start.5 = (bf16[256,256]{1,0:T(8,128)(2,1)S(1)}, bf16[256,256]{1,0:T(8,128)(2,1)}, u32[]{:S(2)}) copy-start(bf16[256,256]{1,0:T(8,128)(2,1)} %param.16) | copy-start | bytes 393220
  187.3 3.0 copy-start.3
  187.3 110.7 %copy-start.1 = (bf16[768,256]{1,0:T(8,128)(2,1)S(1)}, bf16[768,256]{1,0:T(8,128)(2,1)}, u32[]{:S(2)}) copy-start(bf16[768,256]{1,0:T(8,128)(2,1)} %broadcast_select_fusion) | copy-start | bytes 1179652
  187.3 109.1 %all-gather.8.cloned.1.call-start = ((), (), s32[]{:S(2)}) async-start(), calls=%async_computation.10 | async-start | bytes 1966080 | tf_op jit(solution)/shard_map/all_gather | solution.py:52
  187.9 129.1 %all-reduce.7.cloned.1.call-start = ((), (), s32[]{:S(2)}) async-start(), calls=%async_computation.7 | async-start | bytes 524288 | tf_op jit(solution)/shard_map/psum | solution.py:47
  217.2 159.8 %all-reduce.9.cloned.1.call-start = ((), (), s32[]{:S(2)}) async-start(), calls=%async_computation.11 | async-start | bytes 1048576 | tf_op jit(solution)/shard_map/psum | solution.py:69
  378.3 2.0 copy-start.6
Sparse Core Ops, SparseCore 0:
  10.3 40.9 all-gather.3
  52.9 37.1 all-gather.5
  104.9 73.8 reduce-scatter.2
  181.6 35.5 all-reduce.4
  220.0 43.7 reduce-scatter.4
  265.5 30.8 all-gather.7
  298.7 18.2 all-reduce.6
  319.3 57.6 all-reduce.8
